TPU v7x, 32 devices: a whole 2x2x4 slice. The times are simulated.
32 devices in a mesh: pp: 4 (over y, x), cp: 8 (over z, core).
Axes of the slice: x: 2, y: 2, z: 4, core: 2. Of those that a mesh axis runs over, the one named last changes fastest.
Arguments:
- x_in: bfloat16 [4, 1024, 2048], P(None, 'cp'), may hold values from -60 to 80
- norm_gain: float32 [4, 2048], P('pp'), may hold values from 0.5 to 1.5
- w_qkv: bfloat16 [4, 2048, 3072], P('pp', 'cp'), may hold values from -0.13258252 to 1.307771
- w_out: bfloat16 [4, 2048, 2048], P('pp', 'cp'), may hold values from -0.125 to 0.125
- cycle_size: int32 [4], replicated, may hold values from 2 to 8, as said below
- token_pos: int32 [4, 1024], replicated, may hold values from 0 to 1023, as said below
- doc_starts: int32 [4, 16], replicated, may hold values from 0 to 1024, as said below
Outputs:
- layer_outputs: bfloat16 [4, 4, 1024, 2048], P('pp', None, 'cp')
Inputs may be any that keep to these rules, and one draw needn't show every extreme that they name: `cycle_size`: powers of two dividing the devices of cp; some micro-batch has 8 and some has 2. `token_pos`: for a micro-batch with group size r, every aligned block of r * 128 slots holds each position of that block once. `doc_starts`: for a micro-batch with group size r and g below 8 / r, entry 2 g is g * r * 128 and entry 2 g + 1 either lies strictly inside that group's positions or is 1024, so each group holds one or two documents; the remaining entries are 1024.
All inputs are finite; a program needn't handle non-finite values.
Results may differ from a plain program's by a relative error of at most 0.0075.
Values may be sent and summed in bfloat16 or wider, within the bound.
A program may use at most 128 MiB of HBM per device.

v0:
```python
import jax
import jax.numpy as jnp
from jax import lax
from jax.sharding import PartitionSpec as P

HEADS = 16
KV_HEADS = 4
HEAD_DIM = 128
CYCLE_MAX = 8


epsilon = 1e-05
rope_base = 500000.0


def swapped(array, axis, stride):
    return lax.ppermute(array, axis, [(i, i ^ 1 << stride) for i in range(lax.axis_size(axis))])


def from_behind(value, axis, steps):
    count = lax.axis_size(axis)
    leading, last = (max(0, -steps), min(count, count - steps))
    return lax.ppermute(value, axis, [(source, source + steps) for source in range(leading, last)])


def rotate(values, relative):
    half_dim = values.shape[-1] // 2
    frequency_index = jnp.arange(half_dim, dtype=jnp.float32)
    inverse = jnp.power(jnp.float32(rope_base), -2.0 * frequency_index / values.shape[-1])
    angles = relative.astype(jnp.float32)[:, None] * inverse[None, :]
    cosine = jnp.cos(angles)[:, None, :]
    sine_part = jnp.sin(angles)[:, None, :]
    first_half = values[..., :half_dim]
    second_half = values[..., half_dim:]
    return jnp.concatenate(
        [
            first_half * cosine - second_half * sine_part,
            second_half * cosine + first_half * sine_part,
        ],
        axis=-1,
    )


def doc_begin(positions, starts):
    at_or_below = starts[None, :] <= positions[:, None]
    return jnp.max(jnp.where(at_or_below, starts[None, :], 0), axis=1)


def collect_keys(own_piece, device):
    tok_rows, piece_cols = own_piece.shape
    bit_total = CYCLE_MAX.bit_length() - 1
    bit_order = list(reversed(range(bit_total)))
    key_block = own_piece[None]
    for bit_index in bit_order:
        partner = swapped(key_block, "cp", bit_index)
        upper_half = device // (1 << bit_index) % 2 == 1
        key_block = jnp.where(
            upper_half,
            jnp.concatenate([partner, key_block], axis=0),
            jnp.concatenate([key_block, partner], axis=0),
        )
    shaped = key_block.reshape((2,) * bit_total + (tok_rows, piece_cols))
    flipped = tuple(reversed(range(bit_total))) + (bit_total, bit_total + 1)
    key_block = jnp.transpose(shaped, flipped)
    return key_block.reshape(CYCLE_MAX * tok_rows, piece_cols)


def attend_block(queries, key_block, query_pos, key_pos, starts, cycle_devices):
    tok_rows = queries.shape[0]
    key_cols = KV_HEADS * HEAD_DIM
    grouped = queries.reshape(tok_rows, KV_HEADS, HEADS // KV_HEADS, HEAD_DIM)
    key_part = key_block[:, :key_cols].reshape(-1, KV_HEADS, HEAD_DIM)
    value_part = key_block[:, key_cols:].reshape(-1, KV_HEADS, HEAD_DIM)
    scores = jnp.einsum(
        "bkgd,skd->kgbs", grouped, key_part, preferred_element_type=jnp.float32
    ) * HEAD_DIM ** (-0.5)
    span = cycle_devices * tok_rows
    query_begin = doc_begin(query_pos, starts)
    key_begin = doc_begin(key_pos, starts)
    visible = (
        ((query_pos // span)[:, None] == (key_pos // span)[None, :])
        & (query_begin[:, None] == key_begin[None, :])
        & (key_pos[None, :] <= query_pos[:, None])
    )
    scores = jnp.where(visible[None, None], scores, -1e30)
    row_max = jnp.max(scores, axis=-1, keepdims=True)
    weights_exp = jnp.exp(scores - row_max)
    row_sum = jnp.sum(weights_exp, axis=-1, keepdims=True)
    combined = (
        jnp.einsum(
            "kgbs,skd->kgbd",
            weights_exp.astype(jnp.bfloat16),
            value_part,
            preferred_element_type=jnp.float32,
        )
        / row_sum
    )
    return (
        jnp.transpose(combined, (2, 0, 1, 3))
        .reshape(tok_rows, HEADS * HEAD_DIM)
        .astype(jnp.bfloat16)
    )


def body(x_in, norm_gain, w_qkv, w_out, cycle_size, token_pos, doc_starts):
    sections = lax.axis_size("pp")
    section_index = lax.axis_index("pp")
    device = lax.axis_index("cp")
    micro_count, tok_rows, model_width = x_in.shape
    query_cols = HEADS * HEAD_DIM
    key_cols = KV_HEADS * HEAD_DIM
    gain_row = norm_gain[0]
    out_full = None
    qkv_gathered, out_gathered = (
        lax.all_gather(w_qkv, "cp", axis=1, tiled=True),
        lax.all_gather(w_out, "cp", axis=1, tiled=True),
    )
    qkv_full = qkv_gathered[0]
    out_full = out_gathered[0]
    carried = jnp.zeros((tok_rows, model_width), jnp.bfloat16)
    outputs = jnp.zeros((micro_count, tok_rows, model_width), jnp.bfloat16)
    turn_count = micro_count + sections - 1
    for turn_index in range(turn_count):
        offset = turn_index - section_index
        active = (offset >= 0) & (offset < micro_count)
        micro_index = jnp.clip(offset, 0, micro_count - 1)
        fresh_input = lax.dynamic_index_in_dim(x_in, micro_index, 0, keepdims=False)
        hidden = jnp.where(section_index == 0, fresh_input, carried)
        positions = lax.dynamic_index_in_dim(token_pos, micro_index, 0, keepdims=False)
        starts = lax.dynamic_index_in_dim(doc_starts, micro_index, 0, keepdims=False)
        cycle_devices = lax.dynamic_index_in_dim(cycle_size, micro_index, 0, keepdims=False)
        own_pos = lax.dynamic_slice_in_dim(positions, device * tok_rows, tok_rows)

        def front_work(layer_input):
            widened = layer_input.astype(jnp.float32)
            mean_square = jnp.mean(widened * widened, axis=-1, keepdims=True)
            normed = (widened * lax.rsqrt(mean_square + epsilon) * gain_row).astype(jnp.bfloat16)
            projected = jnp.dot(normed, qkv_full, preferred_element_type=jnp.float32)
            relative = own_pos - doc_begin(own_pos, starts)
            queries = rotate(
                projected[:, :query_cols].reshape(tok_rows, HEADS, HEAD_DIM), relative
            ).astype(jnp.bfloat16)
            keys_own = rotate(
                projected[:, query_cols : query_cols + key_cols].reshape(
                    tok_rows, KV_HEADS, HEAD_DIM
                ),
                relative,
            ).astype(jnp.bfloat16)
            values_own = projected[:, query_cols + key_cols :].astype(jnp.bfloat16)
            return (
                queries,
                jnp.concatenate([keys_own.reshape(tok_rows, key_cols), values_own], axis=1),
            )

        def front_empty(layer_input):
            return (
                jnp.zeros((tok_rows, HEADS, HEAD_DIM), jnp.bfloat16),
                jnp.zeros((tok_rows, 2 * key_cols), jnp.bfloat16),
            )

        queries, own_piece = lax.cond(active, front_work, front_empty, hidden)
        key_block = collect_keys(own_piece, device)
        block_start = device // CYCLE_MAX * CYCLE_MAX
        key_pos = lax.dynamic_slice_in_dim(positions, block_start * tok_rows, CYCLE_MAX * tok_rows)
        out_matrix = out_full

        def back_work(layer_input):
            attended = attend_block(queries, key_block, own_pos, key_pos, starts, cycle_devices)
            return (
                layer_input.astype(jnp.float32)
                + jnp.dot(attended, out_matrix, preferred_element_type=jnp.float32)
            ).astype(jnp.bfloat16)

        def back_empty(layer_input):
            return jnp.zeros((tok_rows, model_width), jnp.bfloat16)

        result = lax.cond(active, back_work, back_empty, hidden)
        outputs = jnp.where(
            active, lax.dynamic_update_index_in_dim(outputs, result, micro_index, 0), outputs
        )
        if turn_index + 1 < turn_count:
            carried = from_behind(result, "pp", 1)
    return outputs[None]


def solution(mesh):
    in_specs = (
        P(None, "cp", None),
        P("pp", None),
        P("pp", "cp", None),
        P("pp", "cp", None),
        P(),
        P(),
        P(),
    )
    out_specs = P("pp", None, "cp", None)
    return jax.shard_map(body, mesh=mesh, in_specs=in_specs, out_specs=out_specs, check_vma=False)
```

profile of v0, /device:TPU:31, one launch (start us, length us, event | category | flops | bytes accessed | tf_op | source)
XLA Modules:
  0.0 755.2 jit_solution(12128006746851034836)
XLA Ops:
  12.3 111.9 %all-gather.3.cloned.1.call-done = bf16[1,2048,3072]{2,1,0:T(8,128)(2,1)} async-done(((bf16[1,256,3072]{2,1,0:T(8,128)(2,1)}), bf16[1,2048,3072]{2,1,0:T(8,128)(2,1)}) %all-gather.3.cloned.1.call-update) | async-done | bytes 12582928 | tf_op jit(solution)/shard_map/all_gather | solution.py:115
  124.7 21.3 %collective-permute-done = bf16[1,128,1024]{2,1,0:T(8,128)(2,1)S(1)} collective-permute-done((bf16[1,128,1024]{2,1,0:T(8,128)(2,1)S(1)}, bf16[1,128,1024]{2,1,0:T(8,128)(2,1)S(1)}, u32[]{:S(2)}, u32[]{:S(2)}) %collective-permute-start) | collective-permute-done | bytes 262176 | tf_op jit(solution)/shard_map/ppermute | solution.py:17
  146.2 54.7 %collective-permute-done.1 = bf16[2,128,1024]{2,1,0:T(8,128)(2,1)S(1)} collective-permute-done((bf16[2,128,1024]{2,1,0:T(8,128)(2,1)S(1)}, bf16[2,128,1024]{2,1,0:T(8,128)(2,1)S(1)}, u32[]{:S(2)}, u32[]{:S(2)}) %collective-permute-start.1) | collective-permute-done | bytes 524320 | tf_op jit(solution)/shard_map/ppermute | solution.py:17
  203.0 2.7 collective-permute-done.2
  207.3 4.8 copy.70
  212.0 7.8 %all-gather.5.cloned.1.call-done = bf16[1,2048,2048]{2,1,0:T(8,128)(2,1)} async-done(((bf16[1,256,2048]{2,1,0:T(8,128)(2,1)}), bf16[1,2048,2048]{2,1,0:T(8,128)(2,1)}) %all-gather.5.cloned.1.call-update) | async-done | bytes 8388624 | tf_op jit(solution)/shard_map/all_gather | solution.py:116
  222.3 14.0 %collective-permute-done.3 = bf16[128,2048]{1,0:T(8,128)(2,1)S(1)} collective-permute-done((bf16[128,2048]{1,0:T(8,128)(2,1)}, bf16[128,2048]{1,0:T(8,128)(2,1)S(1)}, u32[]{:S(2)}, u32[]{:S(2)}) %collective-permute-start.3) | collective-permute-done | bytes 524320 | tf_op jit(solution)/shard_map/ppermute | solution.py:23
  237.7 2.9 collective-permute-start.4
  240.6 11.7 %collective-permute-done.4 = bf16[1,128,1024]{2,1,0:T(8,128)(2,1)S(1)} collective-permute-done((bf16[1,128,1024]{2,1,0:T(8,128)(2,1)S(1)}, bf16[1,128,1024]{2,1,0:T(8,128)(2,1)S(1)}, u32[]{:S(2)}, u32[]{:S(2)}) %collective-permute-start.4) | collective-permute-done | bytes 262176 | tf_op jit(solution)/shard_map/ppermute | solution.py:17
  252.5 12.3 %collective-permute-done.5 = bf16[2,128,1024]{2,1,0:T(8,128)(2,1)S(1)} collective-permute-done((bf16[2,128,1024]{2,1,0:T(8,128)(2,1)S(1)}, bf16[2,128,1024]{2,1,0:T(8,128)(2,1)S(1)}, u32[]{:S(2)}, u32[]{:S(2)}) %collective-permute-start.5) | collective-permute-done | bytes 524320 | tf_op jit(solution)/shard_map/ppermute | solution.py:17
  264.9 2.1 collective-permute-start.6
  267.0 2.3 collective-permute-done.6
  271.0 4.7 copy.72
  279.0 13.9 %collective-permute-done.7 = bf16[128,2048]{1,0:T(8,128)(2,1)S(1)} collective-permute-done((bf16[128,2048]{1,0:T(8,128)(2,1)}, bf16[128,2048]{1,0:T(8,128)(2,1)S(1)}, u32[]{:S(2)}, u32[]{:S(2)}) %collective-permute-start.7) | collective-permute-done | bytes 524320 | tf_op jit(solution)/shard_map/ppermute | solution.py:23
  294.5 14.5 %collective-permute-done.8 = bf16[1,128,1024]{2,1,0:T(8,128)(2,1)S(1)} collective-permute-done((bf16[1,128,1024]{2,1,0:T(8,128)(2,1)S(1)}, bf16[1,128,1024]{2,1,0:T(8,128)(2,1)S(1)}, u32[]{:S(2)}, u32[]{:S(2)}) %collective-permute-start.8) | collective-permute-done | bytes 262176 | tf_op jit(solution)/shard_map/ppermute | solution.py:17
  309.1 13.0 %collective-permute-done.9 = bf16[2,128,1024]{2,1,0:T(8,128)(2,1)S(1)} collective-permute-done((bf16[2,128,1024]{2,1,0:T(8,128)(2,1)S(1)}, bf16[2,128,1024]{2,1,0:T(8,128)(2,1)S(1)}, u32[]{:S(2)}, u32[]{:S(2)}) %collective-permute-start.9) | collective-permute-done | bytes 524320 | tf_op jit(solution)/shard_map/ppermute | solution.py:17
  323.6 2.3 collective-permute-done.10
  327.6 4.7 copy.74
  332.3 2.2 conditional.19
  334.6 11.9 %collective-permute-start.11 = (bf16[128,2048]{1,0:T(8,128)(2,1)}, bf16[128,2048]{1,0:T(8,128)(2,1)S(1)}, u32[]{:S(2)}, u32[]{:S(2)}) collective-permute-start(bf16[128,2048]{1,0:T(8,128)(2,1)} %get-tuple-element.681), channel_id=1, source_target_pairs={{0,8},{8,16},{16,24},{1,9},{9,17},{17,25},{2,10},{10,18},{18,26},{... | collective-permute-start | bytes 1572872 | tf_op jit(solution)/shard_map/ppermute | solution.py:23
  346.5 77.3 %collective-permute-done.11 = bf16[128,2048]{1,0:T(8,128)(2,1)S(1)} collective-permute-done((bf16[128,2048]{1,0:T(8,128)(2,1)}, bf16[128,2048]{1,0:T(8,128)(2,1)S(1)}, u32[]{:S(2)}, u32[]{:S(2)}) %collective-permute-start.11) | collective-permute-done | bytes 524320 | tf_op jit(solution)/shard_map/ppermute | solution.py:23
  424.8 9.0 %conditional.20 = (bf16[128,16,128]{2,1,0:T(8,128)(2,1)S(1)}, bf16[1,128,1024]{2,1,0:T(8,128)(2,1)S(1)}) conditional(s32[]{:T(128)} %convert_element_type.311, () %tuple.184, (bf16[128,2048]{1,0:T(8,128)(2,1)S(1)}, f32[1,2048]{1,0:T(1,128)S(1)}, bf16[2048,3072]{1,0:T(8,128)(2,1)}, s32[16]{0:T(128)S(1)}, s32[128]{0:T(128)S(1)}) %tuple.322), branch_computations={%region_30.31_spmd, %region_31.34_spmd} | conditional | flops 1615608192 | bytes 24983120 | solution.py:161
  425.0 6.5 fusion.69
  434.4 14.0 %collective-permute-done.12 = bf16[1,128,1024]{2,1,0:T(8,128)(2,1)S(1)} collective-permute-done((bf16[1,128,1024]{2,1,0:T(8,128)(2,1)S(1)}, bf16[1,128,1024]{2,1,0:T(8,128)(2,1)S(1)}, u32[]{:S(2)}, u32[]{:S(2)}) %collective-permute-start.12) | collective-permute-done | bytes 262176 | tf_op jit(solution)/shard_map/ppermute | solution.py:17
  448.5 13.0 %collective-permute-done.13 = bf16[2,128,1024]{2,1,0:T(8,128)(2,1)S(1)} collective-permute-done((bf16[2,128,1024]{2,1,0:T(8,128)(2,1)S(1)}, bf16[2,128,1024]{2,1,0:T(8,128)(2,1)S(1)}, u32[]{:S(2)}, u32[]{:S(2)}) %collective-permute-start.13) | collective-permute-done | bytes 524320 | tf_op jit(solution)/shard_map/ppermute | solution.py:17
  463.1 2.3 collective-permute-done.14
  467.0 4.7 copy.76
  471.7 18.7 %conditional.21 = (bf16[128,2048]{1,0:T(8,128)(2,1)}, bf16[1,128,2048]{2,1,0:T(8,128)(2,1)}) conditional(s32[]{:T(128)} %convert_element_type.311, () %tuple.183, (bf16[128,2048]{1,0:T(8,128)(2,1)S(1)}, s32[128]{0:T(128)S(1)}, s32[4]{0:T(128)S(1)}, s32[]{:T(128)}, s32[4,1024]{1,0:T(4,128)S(1)}, /*index=5*/s32[16]{0:T(128)S(1)}, ...), branch_computations={%region_34.35_spmd, %region_35.40_spmd} | conditional | flops 2172577792 | bytes 78724880 | solution.py:177
  471.7 2.7 reshape.1320
  474.4 2.7 fusion.165
  483.1 2.1 divide_convert_fusion.3
  491.8 14.8 %collective-permute-done.15 = bf16[128,2048]{1,0:T(8,128)(2,1)S(1)} collective-permute-done((bf16[128,2048]{1,0:T(8,128)(2,1)}, bf16[128,2048]{1,0:T(8,128)(2,1)S(1)}, u32[]{:S(2)}, u32[]{:S(2)}) %collective-permute-start.15) | collective-permute-done | bytes 524320 | tf_op jit(solution)/shard_map/ppermute | solution.py:23
  507.7 9.2 %conditional.22 = (bf16[128,16,128]{2,1,0:T(8,128)(2,1)S(1)}, bf16[1,128,1024]{2,1,0:T(8,128)(2,1)S(1)}) conditional(s32[]{:T(128)} %convert_element_type.312, () %tuple.188, (bf16[128,2048]{1,0:T(8,128)(2,1)S(1)}, f32[1,2048]{1,0:T(1,128)S(1)}, bf16[2048,3072]{1,0:T(8,128)(2,1)}, s32[16]{0:T(128)S(1)}, s32[128]{0:T(128)S(1)}) %tuple.323), branch_computations={%region_40.41_spmd, %region_41.44_spmd} | conditional | flops 1615608192 | bytes 24983120 | solution.py:161
  507.9 6.5 fusion.91
  517.4 14.0 %collective-permute-done.16 = bf16[1,128,1024]{2,1,0:T(8,128)(2,1)S(1)} collective-permute-done((bf16[1,128,1024]{2,1,0:T(8,128)(2,1)S(1)}, bf16[1,128,1024]{2,1,0:T(8,128)(2,1)S(1)}, u32[]{:S(2)}, u32[]{:S(2)}) %collective-permute-start.16) | collective-permute-done | bytes 262176 | tf_op jit(solution)/shard_map/ppermute | solution.py:17
  531.6 13.0 %collective-permute-done.17 = bf16[2,128,1024]{2,1,0:T(8,128)(2,1)S(1)} collective-permute-done((bf16[2,128,1024]{2,1,0:T(8,128)(2,1)S(1)}, bf16[2,128,1024]{2,1,0:T(8,128)(2,1)S(1)}, u32[]{:S(2)}, u32[]{:S(2)}) %collective-permute-start.17) | collective-permute-done | bytes 524320 | tf_op jit(solution)/shard_map/ppermute | solution.py:17
  546.2 2.3 collective-permute-done.18
  550.1 4.7 copy.78
  554.9 18.7 %conditional.23 = (bf16[128,2048]{1,0:T(8,128)(2,1)}, bf16[1,128,2048]{2,1,0:T(8,128)(2,1)}) conditional(s32[]{:T(128)} %convert_element_type.312, () %tuple.187, (bf16[128,2048]{1,0:T(8,128)(2,1)S(1)}, s32[128]{0:T(128)S(1)}, s32[4]{0:T(128)S(1)}, s32[]{:T(128)}, s32[4,1024]{1,0:T(4,128)S(1)}, /*index=5*/s32[16]{0:T(128)S(1)}, ...), branch_computations={%region_44.45_spmd, %region_45.50_spmd} | conditional | flops 2172577792 | bytes 78724880 | solution.py:177
  554.9 2.7 reshape.1326
  557.6 2.7 fusion.166
  566.2 2.1 divide_convert_fusion.4
  574.9 14.8 %collective-permute-done.19 = bf16[128,2048]{1,0:T(8,128)(2,1)S(1)} collective-permute-done((bf16[128,2048]{1,0:T(8,128)(2,1)}, bf16[128,2048]{1,0:T(8,128)(2,1)S(1)}, u32[]{:S(2)}, u32[]{:S(2)}) %collective-permute-start.19) | collective-permute-done | bytes 524320 | tf_op jit(solution)/shard_map/ppermute | solution.py:23
  590.8 9.4 %conditional.24 = (bf16[128,16,128]{2,1,0:T(8,128)(2,1)S(1)}, bf16[1,128,1024]{2,1,0:T(8,128)(2,1)S(1)}) conditional(s32[]{:T(128)} %convert_element_type.313, () %tuple.192, (bf16[128,2048]{1,0:T(8,128)(2,1)S(1)}, f32[1,2048]{1,0:T(1,128)S(1)}, bf16[2048,3072]{1,0:T(8,128)(2,1)}, s32[16]{0:T(128)S(1)}, s32[128]{0:T(128)S(1)}) %tuple.342), branch_computations={%region_50.51_spmd, %region_51.54_spmd} | conditional | flops 1615608192 | bytes 24983120 | solution.py:161
  591.4 6.5 fusion.113
  600.7 14.1 %collective-permute-done.20 = bf16[1,128,1024]{2,1,0:T(8,128)(2,1)S(1)} collective-permute-done((bf16[1,128,1024]{2,1,0:T(8,128)(2,1)S(1)}, bf16[1,128,1024]{2,1,0:T(8,128)(2,1)S(1)}, u32[]{:S(2)}, u32[]{:S(2)}) %collective-permute-start.20) | collective-permute-done | bytes 262176 | tf_op jit(solution)/shard_map/ppermute | solution.py:17
  614.9 13.0 %collective-permute-done.21 = bf16[2,128,1024]{2,1,0:T(8,128)(2,1)S(1)} collective-permute-done((bf16[2,128,1024]{2,1,0:T(8,128)(2,1)S(1)}, bf16[2,128,1024]{2,1,0:T(8,128)(2,1)S(1)}, u32[]{:S(2)}, u32[]{:S(2)}) %collective-permute-start.21) | collective-permute-done | bytes 524320 | tf_op jit(solution)/shard_map/ppermute | solution.py:17
  629.5 2.3 collective-permute-done.22
  633.4 4.7 copy.80
  638.2 18.9 %conditional.25 = (bf16[128,2048]{1,0:T(8,128)(2,1)}, bf16[1,128,2048]{2,1,0:T(8,128)(2,1)}) conditional(s32[]{:T(128)} %convert_element_type.313, () %tuple.191, (bf16[128,2048]{1,0:T(8,128)(2,1)S(1)}, s32[128]{0:T(128)S(1)}, s32[4]{0:T(128)S(1)}, s32[]{:T(128)}, s32[4,1024]{1,0:T(4,128)S(1)}, /*index=5*/s32[16]{0:T(128)S(1)}, ...), branch_computations={%region_54.55_spmd, %region_55.60_spmd} | conditional | flops 2172577792 | bytes 78724880 | solution.py:177
  638.4 2.7 reshape.1332
  641.1 2.7 fusion.167
  649.7 2.1 divide_convert_fusion.5
  658.4 14.8 %collective-permute-done.23 = bf16[128,2048]{1,0:T(8,128)(2,1)S(1)} collective-permute-done((bf16[128,2048]{1,0:T(8,128)(2,1)}, bf16[128,2048]{1,0:T(8,128)(2,1)S(1)}, u32[]{:S(2)}, u32[]{:S(2)}) %collective-permute-start.23) | collective-permute-done | bytes 524320 | tf_op jit(solution)/shard_map/ppermute | solution.py:23
  674.3 9.2 %conditional.26 = (bf16[128,16,128]{2,1,0:T(8,128)(2,1)S(1)}, bf16[1,128,1024]{2,1,0:T(8,128)(2,1)S(1)}) conditional(s32[]{:T(128)} %convert_element_type.314, () %tuple.196, (bf16[128,2048]{1,0:T(8,128)(2,1)S(1)}, f32[1,2048]{1,0:T(1,128)S(1)}, bf16[2048,3072]{1,0:T(8,128)(2,1)}, s32[16]{0:T(128)S(1)}, s32[128]{0:T(128)S(1)}) %tuple.340), branch_computations={%region_60.61_spmd, %region_61.64_spmd} | conditional | flops 1615608192 | bytes 24983120 | solution.py:161
  674.7 6.5 fusion.135
  684.7 13.4 %collective-permute-done.24 = bf16[1,128,1024]{2,1,0:T(8,128)(2,1)S(1)} collective-permute-done((bf16[1,128,1024]{2,1,0:T(8,128)(2,1)S(1)}, bf16[1,128,1024]{2,1,0:T(8,128)(2,1)S(1)}, u32[]{:S(2)}, u32[]{:S(2)}) %collective-permute-start.24) | collective-permute-done | bytes 262176 | tf_op jit(solution)/shard_map/ppermute | solution.py:17
  698.6 12.6 %collective-permute-done.25 = bf16[2,128,1024]{2,1,0:T(8,128)(2,1)S(1)} collective-permute-done((bf16[2,128,1024]{2,1,0:T(8,128)(2,1)S(1)}, bf16[2,128,1024]{2,1,0:T(8,128)(2,1)S(1)}, u32[]{:S(2)}, u32[]{:S(2)}) %collective-permute-start.25) | collective-permute-done | bytes 524320 | tf_op jit(solution)/shard_map/ppermute | solution.py:17
  719.4 26.7 %conditional.27 = (bf16[1,128,2048]{2,1,0:T(8,128)(2,1)}) conditional(s32[]{:T(128)} %convert_element_type.314, () %tuple.195, (bf16[128,2048]{1,0:T(8,128)(2,1)S(1)}, s32[128]{0:T(128)S(1)}, s32[4]{0:T(128)S(1)}, s32[]{:T(128)}, s32[4,1024]{1,0:T(4,128)S(1)}, /*index=5*/s32[16]{0:T(128)S(1)}, bf16[2,2,2,128,1024]{4,3,0,1,2:T(8,128)(2,1)}, ...), branch_computations={%region_64.65_spmd, %region_65.70_spmd} | conditional | flops 2172577792 | bytes 81870600 | solution.py:177
  719.6 6.2 copy.82
  725.8 4.4 reshape.1338
  730.2 3.1 fusion.168
  736.1 2.8 fusion.141
  740.6 2.1 divide_convert_fusion.6
  (253 shorter events, 108.2 us)
Async XLA Ops:
  6.5 117.7 %all-gather.3.cloned.1.call-start = ((), (), s32[]{:S(2)}) async-start(), calls=%async_computation | async-start | bytes 14155776 | tf_op jit(solution)/shard_map/all_gather | solution.py:115
  7.3 212.6 %all-gather.5.cloned.1.call-start = ((), (), s32[]{:S(2)}) async-start(), calls=%async_computation.1 | async-start | bytes 9437184 | tf_op jit(solution)/shard_map/all_gather | solution.py:116
  124.3 21.9 %copy-start.3 = (bf16[128,16,128]{2,1,0:T(8,128)(2,1)}, bf16[128,16,128]{2,1,0:T(8,128)(2,1)S(1)}, u32[]{:S(2)}) copy-start(bf16[128,16,128]{2,1,0:T(8,128)(2,1)S(1)} %get-tuple-element.671) | copy-start | bytes 1572868
  124.3 95.5 %copy-start.16 = (s32[4,1024]{1,0:T(4,128)S(1)}, s32[4,1024]{1,0:T(4,128)}, u32[]{:S(2)}) copy-start(s32[4,1024]{1,0:T(4,128)} %param.40) | copy-start | bytes 49156
  124.3 95.5 %copy-start.21 = (s32[4]{0:T(128)S(1)}, s32[4]{0:T(128)}, u32[]{:S(2)}) copy-start(s32[4]{0:T(128)} %param.39) | copy-start | bytes 52
  124.3 21.7 %collective-permute-start = (bf16[1,128,1024]{2,1,0:T(8,128)(2,1)S(1)}, bf16[1,128,1024]{2,1,0:T(8,128)(2,1)S(1)}, u32[]{:S(2)}, u32[]{:S(2)}) collective-permute-start(bf16[1,128,1024]{2,1,0:T(8,128)(2,1)S(1)} %get-tuple-element.670), channel_id=1, source_target_pairs={{0,4},{1,5},{2,6},{3,7},{4,0},{5,1},{6,2},{7,3},{8,12},{9,13},{10,... | collective-permute-start | bytes 786440 | tf_op jit(solution)/shard_map/ppermute | solution.py:17
  146.1 54.9 %collective-permute-start.1 = (bf16[2,128,1024]{2,1,0:T(8,128)(2,1)S(1)}, bf16[2,128,1024]{2,1,0:T(8,128)(2,1)S(1)}, u32[]{:S(2)}, u32[]{:S(2)}) collective-permute-start(bf16[2,128,1024]{2,1,0:T(8,128)(2,1)S(1)} %maximum_select_fusion.14), channel_id=1, source_target_pairs={{0,2},{1,3},{2,0},{3,1},{4,6},{5,7},{6,4},{7,5},{8,10},{9,11},{10,... | collective-permute-start | bytes 1572872 | tf_op jit(solution)/shard_map/ppermute | solution.py:17
  201.1 4.5 collective-permute-start.2
  219.9 17.5 %copy-start = (f32[1,2048]{1,0:T(1,128)S(1)}, f32[1,2048]{1,0:T(1,128)}, u32[]{:S(2)}) copy-start(f32[1,2048]{1,0:T(1,128)} %param.36) | copy-start | bytes 24580
  220.9 16.4 %copy-start.1 = (bf16[1,128,2048]{2,1,0:T(8,128)(2,1)}, bf16[1,128,2048]{2,1,0:T(8,128)(2,1)S(1)}, u32[]{:S(2)}) copy-start(bf16[1,128,2048]{2,1,0:T(8,128)(2,1)S(1)} %get-tuple-element.672) | copy-start | bytes 1572868
  221.0 15.3 %collective-permute-start.3 = (bf16[128,2048]{1,0:T(8,128)(2,1)}, bf16[128,2048]{1,0:T(8,128)(2,1)S(1)}, u32[]{:S(2)}, u32[]{:S(2)}) collective-permute-start(bf16[128,2048]{1,0:T(8,128)(2,1)} %get-tuple-element.673), channel_id=1, source_target_pairs={{0,8},{8,16},{16,24},{1,9},{9,17},{17,25},{2,10},{10,18},{18,26},{... | collective-permute-start | bytes 1572872 | tf_op jit(solution)/shard_map/ppermute | solution.py:23
  237.7 33.2 %copy-start.5 = (bf16[128,16,128]{2,1,0:T(8,128)(2,1)}, bf16[128,16,128]{2,1,0:T(8,128)(2,1)S(1)}, u32[]{:S(2)}) copy-start(bf16[128,16,128]{2,1,0:T(8,128)(2,1)S(1)} %get-tuple-element.675) | copy-start | bytes 1572868
  237.7 14.6 %collective-permute-start.4 = (bf16[1,128,1024]{2,1,0:T(8,128)(2,1)S(1)}, bf16[1,128,1024]{2,1,0:T(8,128)(2,1)S(1)}, u32[]{:S(2)}, u32[]{:S(2)}) collective-permute-start(bf16[1,128,1024]{2,1,0:T(8,128)(2,1)S(1)} %get-tuple-element.674), channel_id=1, source_target_pairs={{0,4},{1,5},{2,6},{3,7},{4,0},{5,1},{6,2},{7,3},{8,12},{9,13},{10,... | collective-permute-start | bytes 786440 | tf_op jit(solution)/shard_map/ppermute | solution.py:17
  252.4 12.3 %collective-permute-start.5 = (bf16[2,128,1024]{2,1,0:T(8,128)(2,1)S(1)}, bf16[2,128,1024]{2,1,0:T(8,128)(2,1)S(1)}, u32[]{:S(2)}, u32[]{:S(2)}) collective-permute-start(bf16[2,128,1024]{2,1,0:T(8,128)(2,1)S(1)} %maximum_select_fusion.15), channel_id=1, source_target_pairs={{0,2},{1,3},{2,0},{3,1},{4,6},{5,7},{6,4},{7,5},{8,10},{9,11},{10,... | collective-permute-start | bytes 1572872 | tf_op jit(solution)/shard_map/ppermute | solution.py:17
  264.9 4.4 collective-permute-start.6
  277.7 15.2 %collective-permute-start.7 = (bf16[128,2048]{1,0:T(8,128)(2,1)}, bf16[128,2048]{1,0:T(8,128)(2,1)S(1)}, u32[]{:S(2)}, u32[]{:S(2)}) collective-permute-start(bf16[128,2048]{1,0:T(8,128)(2,1)} %get-tuple-element.677), channel_id=1, source_target_pairs={{0,8},{8,16},{16,24},{1,9},{9,17},{17,25},{2,10},{10,18},{18,26},{... | collective-permute-start | bytes 1572872 | tf_op jit(solution)/shard_map/ppermute | solution.py:23
  294.4 14.5 %collective-permute-start.8 = (bf16[1,128,1024]{2,1,0:T(8,128)(2,1)S(1)}, bf16[1,128,1024]{2,1,0:T(8,128)(2,1)S(1)}, u32[]{:S(2)}, u32[]{:S(2)}) collective-permute-start(bf16[1,128,1024]{2,1,0:T(8,128)(2,1)S(1)} %get-tuple-element.678), channel_id=1, source_target_pairs={{0,4},{1,5},{2,6},{3,7},{4,0},{5,1},{6,2},{7,3},{8,12},{9,13},{10,... | collective-permute-start | bytes 786440 | tf_op jit(solution)/shard_map/ppermute | solution.py:17
  309.0 13.1 %collective-permute-start.9 = (bf16[2,128,1024]{2,1,0:T(8,128)(2,1)S(1)}, bf16[2,128,1024]{2,1,0:T(8,128)(2,1)S(1)}, u32[]{:S(2)}, u32[]{:S(2)}) collective-permute-start(bf16[2,128,1024]{2,1,0:T(8,128)(2,1)S(1)} %maximum_select_fusion.16), channel_id=1, source_target_pairs={{0,2},{1,3},{2,0},{3,1},{4,6},{5,7},{6,4},{7,5},{8,10},{9,11},{10,... | collective-permute-start | bytes 1572872 | tf_op jit(solution)/shard_map/ppermute | solution.py:17
  322.2 3.7 collective-permute-start.10
  334.6 89.2 %collective-permute-start.11 = (bf16[128,2048]{1,0:T(8,128)(2,1)}, bf16[128,2048]{1,0:T(8,128)(2,1)S(1)}, u32[]{:S(2)}, u32[]{:S(2)}) collective-permute-start(bf16[128,2048]{1,0:T(8,128)(2,1)} %get-tuple-element.681), channel_id=1, source_target_pairs={{0,8},{8,16},{16,24},{1,9},{9,17},{17,25},{2,10},{10,18},{18,26},{... | collective-permute-start | bytes 1572872 | tf_op jit(solution)/shard_map/ppermute | solution.py:23
  433.8 14.5 %collective-permute-start.12 = (bf16[1,128,1024]{2,1,0:T(8,128)(2,1)S(1)}, bf16[1,128,1024]{2,1,0:T(8,128)(2,1)S(1)}, u32[]{:S(2)}, u32[]{:S(2)}) collective-permute-start(bf16[1,128,1024]{2,1,0:T(8,128)(2,1)S(1)} %get-tuple-element.682), channel_id=1, source_target_pairs={{0,4},{1,5},{2,6},{3,7},{4,0},{5,1},{6,2},{7,3},{8,12},{9,13},{10,... | collective-permute-start | bytes 786440 | tf_op jit(solution)/shard_map/ppermute | solution.py:17
  448.4 13.1 %collective-permute-start.13 = (bf16[2,128,1024]{2,1,0:T(8,128)(2,1)S(1)}, bf16[2,128,1024]{2,1,0:T(8,128)(2,1)S(1)}, u32[]{:S(2)}, u32[]{:S(2)}) collective-permute-start(bf16[2,128,1024]{2,1,0:T(8,128)(2,1)S(1)} %maximum_select_fusion.17), channel_id=1, source_target_pairs={{0,2},{1,3},{2,0},{3,1},{4,6},{5,7},{6,4},{7,5},{8,10},{9,11},{10,... | collective-permute-start | bytes 1572872 | tf_op jit(solution)/shard_map/ppermute | solution.py:17
  461.6 3.7 collective-permute-start.14
  479.8 3.3 copy-start.12
  483.0 2.2 slice-start.6
  483.1 3.5 slice-start.7
  490.5 16.1 %collective-permute-start.15 = (bf16[128,2048]{1,0:T(8,128)(2,1)}, bf16[128,2048]{1,0:T(8,128)(2,1)S(1)}, u32[]{:S(2)}, u32[]{:S(2)}) collective-permute-start(bf16[128,2048]{1,0:T(8,128)(2,1)} %get-tuple-element.685), channel_id=1, source_target_pairs={{0,8},{8,16},{16,24},{1,9},{9,17},{17,25},{2,10},{10,18},{18,26},{... | collective-permute-start | bytes 1572872 | tf_op jit(solution)/shard_map/ppermute | solution.py:23
  516.9 14.6 %collective-permute-start.16 = (bf16[1,128,1024]{2,1,0:T(8,128)(2,1)S(1)}, bf16[1,128,1024]{2,1,0:T(8,128)(2,1)S(1)}, u32[]{:S(2)}, u32[]{:S(2)}) collective-permute-start(bf16[1,128,1024]{2,1,0:T(8,128)(2,1)S(1)} %get-tuple-element.686), channel_id=1, source_target_pairs={{0,4},{1,5},{2,6},{3,7},{4,0},{5,1},{6,2},{7,3},{8,12},{9,13},{10,... | collective-permute-start | bytes 786440 | tf_op jit(solution)/shard_map/ppermute | solution.py:17
  531.5 13.1 %collective-permute-start.17 = (bf16[2,128,1024]{2,1,0:T(8,128)(2,1)S(1)}, bf16[2,128,1024]{2,1,0:T(8,128)(2,1)S(1)}, u32[]{:S(2)}, u32[]{:S(2)}) collective-permute-start(bf16[2,128,1024]{2,1,0:T(8,128)(2,1)S(1)} %maximum_select_fusion.18), channel_id=1, source_target_pairs={{0,2},{1,3},{2,0},{3,1},{4,6},{5,7},{6,4},{7,5},{8,10},{9,11},{10,... | collective-permute-start | bytes 1572872 | tf_op jit(solution)/shard_map/ppermute | solution.py:17
  544.7 3.7 collective-permute-start.18
  554.8 35.9 %copy-start.18 = (s32[128]{0:T(128)S(1)}, s32[128]{0:T(128)}, u32[]{:S(2)}) copy-start(s32[128]{0:T(128)} %get-tuple-element.956) | copy-start | bytes 1540
  554.9 35.9 %copy-start.20 = (s32[16]{0:T(128)S(1)}, s32[16]{0:T(128)}, u32[]{:S(2)}) copy-start(s32[16]{0:T(128)} %get-tuple-element.968) | copy-start | bytes 196
  562.9 3.3 copy-start.13
  566.2 2.2 slice-start.8
  566.2 3.5 slice-start.9
  573.6 16.1 %collective-permute-start.19 = (bf16[128,2048]{1,0:T(8,128)(2,1)}, bf16[128,2048]{1,0:T(8,128)(2,1)S(1)}, u32[]{:S(2)}, u32[]{:S(2)}) collective-permute-start(bf16[128,2048]{1,0:T(8,128)(2,1)} %get-tuple-element.689), channel_id=1, source_target_pairs={{0,8},{8,16},{16,24},{1,9},{9,17},{17,25},{2,10},{10,18},{18,26},{... | collective-permute-start | bytes 1572872 | tf_op jit(solution)/shard_map/ppermute | solution.py:23
  600.2 14.6 %collective-permute-start.20 = (bf16[1,128,1024]{2,1,0:T(8,128)(2,1)S(1)}, bf16[1,128,1024]{2,1,0:T(8,128)(2,1)S(1)}, u32[]{:S(2)}, u32[]{:S(2)}) collective-permute-start(bf16[1,128,1024]{2,1,0:T(8,128)(2,1)S(1)} %get-tuple-element.690), channel_id=1, source_target_pairs={{0,4},{1,5},{2,6},{3,7},{4,0},{5,1},{6,2},{7,3},{8,12},{9,13},{10,... | collective-permute-start | bytes 786440 | tf_op jit(solution)/shard_map/ppermute | solution.py:17
  614.8 13.1 %collective-permute-start.21 = (bf16[2,128,1024]{2,1,0:T(8,128)(2,1)S(1)}, bf16[2,128,1024]{2,1,0:T(8,128)(2,1)S(1)}, u32[]{:S(2)}, u32[]{:S(2)}) collective-permute-start(bf16[2,128,1024]{2,1,0:T(8,128)(2,1)S(1)} %maximum_select_fusion.19), channel_id=1, source_target_pairs={{0,2},{1,3},{2,0},{3,1},{4,6},{5,7},{6,4},{7,5},{8,10},{9,11},{10,... | collective-permute-start | bytes 1572872 | tf_op jit(solution)/shard_map/ppermute | solution.py:17
  628.0 3.7 collective-permute-start.22
  638.1 36.1 %copy-start.17 = (s32[128]{0:T(128)S(1)}, s32[128]{0:T(128)}, u32[]{:S(2)}) copy-start(s32[128]{0:T(128)} %get-tuple-element.955) | copy-start | bytes 1540
  638.2 36.1 %copy-start.19 = (s32[16]{0:T(128)S(1)}, s32[16]{0:T(128)}, u32[]{:S(2)}) copy-start(s32[16]{0:T(128)} %get-tuple-element.962) | copy-start | bytes 196
  646.4 3.3 copy-start.14
  649.7 2.2 slice-start.10
  649.7 3.5 slice-start.11
  657.1 16.1 %collective-permute-start.23 = (bf16[128,2048]{1,0:T(8,128)(2,1)}, bf16[128,2048]{1,0:T(8,128)(2,1)S(1)}, u32[]{:S(2)}, u32[]{:S(2)}) collective-permute-start(bf16[128,2048]{1,0:T(8,128)(2,1)} %get-tuple-element.693), channel_id=1, source_target_pairs={{0,8},{8,16},{16,24},{1,9},{9,17},{17,25},{2,10},{10,18},{18,26},{... | collective-permute-start | bytes 1572872 | tf_op jit(solution)/shard_map/ppermute | solution.py:23
  674.3 10.3 %copy-start.2 = (bf16[1,128,2048]{2,1,0:T(8,128)(2,1)S(1)}, bf16[1,128,2048]{2,1,0:T(8,128)(2,1)}, u32[]{:S(2)}) copy-start(bf16[1,128,2048]{2,1,0:T(8,128)(2,1)} %copy-done.1) | copy-start | bytes 1572868
  683.5 0.8 copy-start.7
  683.5 14.6 %collective-permute-start.24 = (bf16[1,128,1024]{2,1,0:T(8,128)(2,1)S(1)}, bf16[1,128,1024]{2,1,0:T(8,128)(2,1)S(1)}, u32[]{:S(2)}, u32[]{:S(2)}) collective-permute-start(bf16[1,128,1024]{2,1,0:T(8,128)(2,1)S(1)} %get-tuple-element.694), channel_id=1, source_target_pairs={{0,4},{1,5},{2,6},{3,7},{4,0},{5,1},{6,2},{7,3},{8,12},{9,13},{10,... | collective-permute-start | bytes 786440 | tf_op jit(solution)/shard_map/ppermute | solution.py:17
  698.1 13.1 %collective-permute-start.25 = (bf16[2,128,1024]{2,1,0:T(8,128)(2,1)S(1)}, bf16[2,128,1024]{2,1,0:T(8,128)(2,1)S(1)}, u32[]{:S(2)}, u32[]{:S(2)}) collective-permute-start(bf16[2,128,1024]{2,1,0:T(8,128)(2,1)S(1)} %maximum_select_fusion.20), channel_id=1, source_target_pairs={{0,2},{1,3},{2,0},{3,1},{4,6},{5,7},{6,4},{7,5},{8,10},{9,11},{10,... | collective-permute-start | bytes 1572872 | tf_op jit(solution)/shard_map/ppermute | solution.py:17
  698.4 21.0 %copy-start.8 = (bf16[128,16,128]{2,1,0:T(8,128)(2,1)S(1)}, bf16[128,16,128]{2,1,0:T(8,128)(2,1)}, u32[]{:S(2)}) copy-start(bf16[128,16,128]{2,1,0:T(8,128)(2,1)} %copy-done.7) | copy-start | bytes 1572868
  711.3 6.4 collective-permute-start.26
  736.0 4.5 copy-start.15
  740.6 2.2 slice-start.12
  740.6 3.5 slice-start.13
Sparse Core Ops, SparseCore 0:
  9.0 115.1 all-gather.2
  125.8 94.0 all-gather.4
where the time goes:
time: 763 us; the launch traced here: 755 us
  waiting for transfers between devices  519 us (68%)
  local copies, waits for them, and re-layouts  83.7 us (11%)
  matrix products  49.9 us (7%)
  other arithmetic  46.4 us (6%)
  starting transfers between devices  35.3 us (5%)
  between operations  14.3 us (2%)
    ppermute x21, waiting for transfers between devices, swapped(): lax.ppermute(array, axis, [(i, i ^ 1 << stride) for i in range(lax.axis_s...  248 us
    ppermute x6, waiting for transfers between devices, from_behind(): lax.ppermute(value, axis, [(source, source + steps) for source in range(l...  150 us
    all_gather x1, waiting for transfers between devices, body(): lax.all_gather(w_qkv, 'cp', axis=1, tiled=True)  112 us
    select_n x6, local copies, waits for them, and re-layouts, collect_keys(): jnp.where(upper_half, jnp.concatenate([partner, key_block], axis=0), jnp....  28.5 us
    dot_general x4, matrix products, front_work(): projected = jnp.dot(normed, qkv_full, preferred_element_type=jnp.float32)  26 us
    ppermute x6, starting transfers between devices, from_behind(): lax.ppermute(value, axis, [(source, source + steps) for source in range(l...  18.3 us
    ppermute x21, starting transfers between devices, swapped(): lax.ppermute(array, axis, [(i, i ^ 1 << stride) for i in range(lax.axis_s...  17 us
  transfers between devices with their start and end apart: 29, of which 28 were waited for; matrix products, arithmetic and copies ran while one was open for 2% of the time, Pallas kernels for 0%

commit v1 on v0

v1 whole, which is shorter than its diff:
```python
import functools
import math

import jax
import jax.numpy as jnp
from jax import lax
from jax.experimental import pallas as pl
from jax.experimental.pallas import tpu as pltpu
from jax.sharding import PartitionSpec as P

HEADS = 16
KV_HEADS = 4
HEAD_DIM = 128
CYCLE_MAX = 8
CORES = 2
TILE = 256

epsilon = 1e-05
rope_base = 500000.0
MESH = pl.DeviceIdType.MESH


def kernel(
    chips, sections, x_ref, gain_ref, wq_in, wo_in, cos_ref, sin_ref, pos_q, code_q, pos_k, code_k,
    out_ref,
    wq, wo, hid, nrm, qs, kv, att, res, bias,
    w_swap_s, w_swap_r, w_right_s, w_right_r, w_left_s, w_left_r,
    x_s, x_r, loc, hop_s, hop_r, relay_s, relay_r, kv_s, kv_r, att_s, att_r, o_s, o_r,
):
    micro, tok, width = x_ref.shape
    rows = wq_in.shape[1]
    half = width // 2
    q_cols = HEADS // CORES * HEAD_DIM
    kv_cols = KV_HEADS // CORES * HEAD_DIM
    heads = HEADS // CORES
    per_kv = HEADS // KV_HEADS
    peers = CYCLE_MAX // CORES
    tiles = half // TILE
    section = lax.axis_index("pp")
    cp = lax.axis_index("cp")
    chip = cp // CORES
    core = cp % CORES
    partner = {"cp": chip * CORES + 1 - core}
    place = chip % peers
    base = chip - place
    first = section == 0
    last = section == sections - 1

    def remote(src, dst, s, r, device):
        return pltpu.make_async_remote_copy(
            src_ref=src, dst_ref=dst, send_sem=s, recv_sem=r, device_id=device, device_id_type=MESH
        )

    def block(w, index, count):
        return w.at[pl.ds(pl.multiple_of(index * rows, rows), count * rows), :]

    weights = ((wq_in, wq), (wo_in, wo))

    def swap(a):
        src, w = weights[a]
        return remote(src.at[1 - core], block(w, cp, 1), w_swap_s.at[a], w_swap_r.at[a], partner)

    def swap_in(a):
        src, w = weights[a]
        there = chip * CORES + 1 - core
        return remote(src.at[core], block(w, there, 1), w_swap_s.at[a], w_swap_r.at[a], partner)

    def right(a, index):
        piece = block(weights[a][1], index * CORES, CORES)
        return remote(piece, piece, w_right_s.at[a, index], w_right_r.at[a, index],
                      {"cp": (chip + 1) * CORES + core})

    def left(a, index):
        piece = block(weights[a][1], index * CORES, CORES)
        return remote(piece, piece, w_left_s.at[a, index], w_left_r.at[a, index],
                      {"cp": (chip - 1) * CORES + core})

    def own(a):
        src, w = weights[a]
        return pltpu.make_async_copy(src.at[core], block(w, cp, 1), loc.at[a])

    def send_own(a):
        @pl.when(chip < chips - 1)
        def _():
            right(a, chip).start()

        @pl.when(chip > 0)
        def _():
            left(a, chip).start()

    def relay_weights(a):
        def step(i, carry):
            @pl.when(i <= chip)
            def _():
                right(a, chip - i).wait_recv()

                @pl.when(chip < chips - 1)
                def _():
                    right(a, chip - i).start()

            @pl.when(chip + i <= chips - 1)
            def _():
                left(a, chip + i).wait_recv()

                @pl.when(chip > 0)
                def _():
                    left(a, chip + i).start()

            return carry

        lax.fori_loop(1, chips, step, 0)

    def finish_weights(a):
        swap(a).wait_send()

        def step(i, carry):
            @pl.when((i <= chip) & (chip < chips - 1))
            def _():
                right(a, i).wait_send()

            @pl.when((i >= chip) & (chip > 0))
            def _():
                left(a, i).wait_send()

            return carry

        lax.fori_loop(0, chips, step, 0)

    own_rows = pl.ds(pl.multiple_of(core * tok, tok), tok)
    other_rows = pl.ds(pl.multiple_of((1 - core) * tok, tok), tok)

    def x_local(m, h):
        return pltpu.make_async_copy(
            x_ref.at[m, :, pl.ds(h * half, half)], hid.at[m, h, own_rows, :], loc.at[2 + m * 2 + h])

    def x_send(m, h):
        return remote(x_ref.at[m, :, pl.ds(h * half, half)], hid.at[m, h, own_rows, :],
                      x_s.at[m, h], x_r.at[m, h], partner)

    def x_wait(m, h):
        piece = hid.at[m, h, other_rows, :]
        return remote(piece, piece, x_s.at[m, h], x_r.at[m, h], partner)

    def cols(t):
        return pl.ds(pl.multiple_of(t * TILE, TILE), TILE)

    def hop(m, t):
        return remote(res.at[m, :, cols(t)], hid.at[m, core, :, cols(t)],
                      hop_s.at[m, t], hop_r.at[m, t], {"pp": section + 1})

    def relay(m, t):
        return remote(hid.at[m, core, :, cols(t)], hid.at[m, core, :, cols(t)],
                      relay_s.at[m, t], relay_r.at[m, t], partner)

    def relay_in(m, t):
        piece = hid.at[m, 1 - core, :, cols(t)]
        return remote(piece, piece, relay_s.at[m, t], relay_r.at[m, t], partner)

    def kv_send(m, d):
        there = lax.rem(place + d, peers)
        return remote(kv.at[m, place], kv.at[m, place], kv_s.at[m, d - 1], kv_r.at[m, d - 1],
                      {"cp": (base + there) * CORES + core})

    def kv_in(m, d):
        source = lax.rem(place - d + peers, peers)
        return remote(kv.at[m, source], kv.at[m, source], kv_s.at[m, d - 1], kv_r.at[m, d - 1],
                      {"cp": (base + source) * CORES + core})

    def att_send(m, g):
        c = pl.ds(g * per_kv * HEAD_DIM, per_kv * HEAD_DIM)
        return remote(att.at[m, core, :, c], att.at[m, core, :, c], att_s.at[m, g], att_r.at[m, g], partner)

    def att_in(m, g):
        c = pl.ds(g * per_kv * HEAD_DIM, per_kv * HEAD_DIM)
        piece = att.at[m, 1 - core, :, c]
        return remote(piece, piece, att_s.at[m, g], att_r.at[m, g], partner)

    def out_send(m):
        return remote(res.at[m, other_rows, :], out_ref.at[m, :, pl.ds(pl.multiple_of(core * half, half), half)],
                      o_s.at[m], o_r.at[m], partner)

    def out_in(m):
        return remote(res.at[m, own_rows, :],
                      out_ref.at[m, :, pl.ds(pl.multiple_of((1 - core) * half, half), half)],
                      o_s.at[m], o_r.at[m], partner)

    swap(0).start()
    swap(1).start()
    own(0).start()
    own(1).start()
    own(0).wait()
    swap_in(0).wait_recv()
    send_own(0)

    @pl.when(first)
    def _():
        for m in range(micro):
            for h in range(2):
                x_send(m, h).start()
                x_local(m, h).start()

    own(1).wait()
    swap_in(1).wait_recv()
    relay_weights(0)
    send_own(1)

    def rope(values, m):
        return values * cos_ref[m] + pltpu.roll(values, HEAD_DIM // 2, 1) * sin_ref[m]

    def front(m):
        @pl.when(first)
        def _():
            for h in range(2):
                x_local(m, h).wait()
                x_wait(m, h).wait_recv()

        @pl.when(section > 0)
        def _():
            for t in range(tiles):
                hop(m, t).wait_recv()
                relay(m, t).start()
            for t in range(tiles):
                relay_in(m, t).wait_recv()

        low = hid[m, 0].astype(jnp.float32)
        high = hid[m, 1].astype(jnp.float32)
        total = jnp.sum(low * low, axis=1, keepdims=True) + jnp.sum(high * high, axis=1, keepdims=True)
        scale = lax.rsqrt(total / width + epsilon)
        nrm[:, :half] = (low * scale * gain_ref[:, :half]).astype(jnp.bfloat16)
        nrm[:, half:] = (high * scale * gain_ref[:, half:]).astype(jnp.bfloat16)
        keys = jnp.dot(nrm[...], wq[:, q_cols : q_cols + kv_cols], preferred_element_type=jnp.float32)
        for g in range(KV_HEADS // CORES):
            c = slice(g * HEAD_DIM, (g + 1) * HEAD_DIM)
            kv[m, place, :, c] = rope(keys[:, c], m).astype(jnp.bfloat16)
        values = jnp.dot(nrm[...], wq[:, q_cols + kv_cols :], preferred_element_type=jnp.float32)
        kv[m, place, :, kv_cols:] = values.astype(jnp.bfloat16)
        for d in range(1, peers):
            kv_send(m, d).start()

        def q_tile(t, carry):
            part = jnp.dot(nrm[...], wq[:, cols(t)], preferred_element_type=jnp.float32)
            for g in range(TILE // HEAD_DIM):
                c = slice(g * HEAD_DIM, (g + 1) * HEAD_DIM)
                qs[m, t * (TILE // HEAD_DIM) + g] = rope(part[:, c], m).astype(jnp.bfloat16)
            return carry

        lax.fori_loop(0, q_cols // TILE, q_tile, 0)

    factor = HEAD_DIM ** (-0.5) * math.log2(math.e)

    def back(m):
        visible = (code_q[m] == code_k[m]) & (pos_k[m] <= pos_q[m])
        bias[...] = jnp.where(visible, 0.0, -1e30).astype(jnp.float32)
        for d in range(1, peers):
            kv_in(m, d).wait_recv()
        for g in range(KV_HEADS // CORES):
            c = slice(g * HEAD_DIM, (g + 1) * HEAD_DIM)
            v = slice(kv_cols + g * HEAD_DIM, kv_cols + (g + 1) * HEAD_DIM)
            for j in range(per_kv):
                h = g * per_kv + j
                key_block = kv[m, :, :, c].reshape(peers * CORES * tok, HEAD_DIM)
                value_block = kv[m, :, :, v].reshape(peers * CORES * tok, HEAD_DIM)
                scores = lax.dot_general(
                    qs[m, h], key_block, (((1,), (1,)), ((), ())), preferred_element_type=jnp.float32
                ) + bias[...]
                top = jnp.max(scores, axis=1, keepdims=True)
                weights_exp = jnp.exp2((scores - top) * factor)
                row_sum = jnp.sum(weights_exp, axis=1, keepdims=True)
                combined = jnp.dot(
                    weights_exp.astype(jnp.bfloat16), value_block, preferred_element_type=jnp.float32
                )
                att[m, core, :, h * HEAD_DIM : (h + 1) * HEAD_DIM] = (combined / row_sum).astype(jnp.bfloat16)
            att_send(m, g).start()

        @pl.when(m == 0)
        def _():
            relay_weights(1)

        for g in range(KV_HEADS // CORES):
            att_in(m, g).wait_recv()

        def out_tile(t, carry):
            total = jnp.dot(att[m, 0], wo[:half, cols(t)], preferred_element_type=jnp.float32)
            total += jnp.dot(att[m, 1], wo[half:, cols(t)], preferred_element_type=jnp.float32)
            result = (hid[m, core, :, cols(t)].astype(jnp.float32) + total).astype(jnp.bfloat16)
            res[m, :, cols(t)] = result

            @pl.when(section < sections - 1)
            def _():
                hop(m, t).start()

            place_cols = pl.ds(pl.multiple_of(core * half + t * TILE, TILE), TILE)
            out_ref[m, :, place_cols] = res[m, own_rows, cols(t)]
            return carry

        lax.fori_loop(0, tiles, out_tile, 0)
        out_send(m).start()

    def turn(i, carry):
        @pl.when(i < micro)
        def _():
            front(i)

        @pl.when(i > 0)
        def _():
            back(i - 1)

        return carry

    lax.fori_loop(0, micro + 1, turn, 0)

    finish_weights(0)
    finish_weights(1)

    def finish(m, carry):
        @pl.when(first)
        def _():
            for h in range(2):
                x_send(m, h).wait_send()

        @pl.when(section > 0)
        def _():
            for t in range(tiles):
                relay(m, t).wait_send()

        @pl.when(section < sections - 1)
        def _():
            for t in range(tiles):
                hop(m, t).wait_send()

        for d in range(1, peers):
            kv_send(m, d).wait_send()
        for g in range(KV_HEADS // CORES):
            att_send(m, g).wait_send()
        out_send(m).wait_send()
        out_in(m).wait_recv()
        return carry

    lax.fori_loop(0, micro, finish, 0)


def doc_begin(positions, starts):
    at_or_below = starts[:, None, :] <= positions[:, :, None]
    return jnp.max(jnp.where(at_or_below, starts[:, None, :], 0), axis=2)


def body(x_in, norm_gain, w_qkv, w_out, cycle_size, token_pos, doc_starts):
    sections = lax.axis_size("pp")
    chips = lax.axis_size("cp") // CORES
    device = lax.axis_index("cp")
    micro, tok, width = x_in.shape
    rows = w_qkv.shape[1]
    total_tokens = token_pos.shape[1]
    half = width // 2
    query_cols = HEADS * HEAD_DIM
    key_cols = KV_HEADS * HEAD_DIM
    window = CYCLE_MAX * tok
    pair = CORES * tok

    block_start = device // CYCLE_MAX * window
    key_pos = lax.dynamic_slice_in_dim(token_pos, block_start, window, 1)
    key_begin = doc_begin(key_pos, doc_starts)
    key_code = key_pos // (cycle_size * tok)[:, None] * (total_tokens + 1) + key_begin
    inside = device % CYCLE_MAX // CORES * pair
    query_pos = lax.dynamic_slice_in_dim(key_pos, inside, pair, 1)
    query_begin = lax.dynamic_slice_in_dim(key_begin, inside, pair, 1)
    query_code = lax.dynamic_slice_in_dim(key_code, inside, pair, 1)
    frequency_index = jnp.arange(HEAD_DIM // 2, dtype=jnp.float32)
    inverse = jnp.power(jnp.float32(rope_base), -2.0 * frequency_index / HEAD_DIM)
    angles = (query_pos - query_begin).astype(jnp.float32)[:, :, None] * inverse
    cosine, sine = jnp.cos(angles), jnp.sin(angles)
    cos_full = jnp.concatenate([cosine, cosine], axis=-1)
    sin_full = jnp.concatenate([-sine, sine], axis=-1)

    def split(array):
        return jnp.stack(jnp.split(array, CORES, axis=1))

    wq_split = jnp.concatenate(
        [
            split(w_qkv[0][:, :query_cols]),
            split(w_qkv[0][:, query_cols : query_cols + key_cols]),
            split(w_qkv[0][:, query_cols + key_cols :]),
        ],
        axis=2,
    )
    wo_split = split(w_out[0])

    peers = CYCLE_MAX // CORES
    tiles = half // TILE
    bf = jnp.bfloat16
    dma = pltpu.SemaphoreType.DMA
    vmem = pl.BlockSpec(memory_space=pltpu.VMEM)
    outputs = pl.pallas_call(
        functools.partial(kernel, chips, sections),
        out_shape=jax.ShapeDtypeStruct((micro, tok, width), bf),
        in_specs=[vmem] * 10,
        out_specs=vmem,
        scratch_shapes=[
            pltpu.VMEM((width, wq_split.shape[2]), bf),
            pltpu.VMEM((query_cols, half), bf),
            pltpu.VMEM((micro, 2, pair, half), bf),
            pltpu.VMEM((pair, width), bf),
            pltpu.VMEM((micro, HEADS // CORES, pair, HEAD_DIM), bf),
            pltpu.VMEM((micro, peers, pair, 2 * key_cols // CORES), bf),
            pltpu.VMEM((micro, CORES, pair, query_cols // CORES), bf),
            pltpu.VMEM((micro, pair, half), bf),
            pltpu.VMEM((pair, window), jnp.float32),
            dma((2,)), dma((2,)),
            dma((2, chips)), dma((2, chips)), dma((2, chips)), dma((2, chips)),
            dma((micro, 2)), dma((micro, 2)),
            dma((2 + 2 * micro,)),
            dma((micro, tiles)), dma((micro, tiles)),
            dma((micro, tiles)), dma((micro, tiles)),
            dma((micro, peers - 1)), dma((micro, peers - 1)),
            dma((micro, KV_HEADS // CORES)), dma((micro, KV_HEADS // CORES)),
            dma((micro,)), dma((micro,)),
        ],
        compiler_params=pltpu.CompilerParams(has_side_effects=True, vmem_limit_bytes=60 * 1024 * 1024),
    )(
        x_in, norm_gain, wq_split, wo_split, cos_full, sin_full,
        query_pos[:, :, None], query_code[:, :, None], key_pos[:, None, :], key_code[:, None, :],
    )
    return outputs[None]


def solution(mesh):
    in_specs = (
        P(None, "cp", None),
        P("pp", None),
        P("pp", "cp", None),
        P("pp", "cp", None),
        P(),
        P(),
        P(),
    )
    out_specs = P("pp", None, "cp", None)
    return jax.shard_map(body, mesh=mesh, in_specs=in_specs, out_specs=out_specs, check_vma=False)
```

time: 763 us -> 613 us (0.80)
  Pallas kernels: 0 us -> 594 us
  waiting for transfers between devices: 519 us -> 0 us
  local copies, waits for them, and re-layouts: 83.7 us -> 8.88 us
  matrix products: 49.9 us -> 0 us
  other arithmetic: 46.4 us -> 9.09 us
  starting transfers between devices: 35.3 us -> 0 us
  between operations: 14.3 us -> 0.07 us
    pallas_call x0 -> x1, Pallas kernels: none -> 594 us  [body(): pl.pallas_call(functools.partial(kernel, chips, sections), out_shape=jax....]
    ppermute x27 -> x0, waiting for transfers between devices: 398 us -> none  [the longest x21 248 us: swapped(): lax.ppermute(array, axis, [(i, i ^ 1 << stride) for i in range(lax.axis_s...]
    all_gather x2 -> x0, waiting for transfers between devices: 120 us -> none  [the longest x1 112 us: body(): lax.all_gather(w_qkv, 'cp', axis=1, tiled=True)]
    dot_general x16 -> x0, matrix products: 49.9 us -> none  [the longest x4 26 us: front_work(): projected = jnp.dot(normed, qkv_full, preferred_element_type=jnp.float32)]
    ppermute x27 -> x0, starting transfers between devices: 35.3 us -> none  [the longest x6 18.3 us: from_behind(): lax.ppermute(value, axis, [(source, source + steps) for source in range(l...]
    select_n x6 -> x0, local copies, waits for them, and re-layouts: 28.5 us -> none  [collect_keys(): jnp.where(upper_half, jnp.concatenate([partner, key_block], axis=0), jnp....]
    select_n x43 -> x0, other arithmetic: 27.9 us -> none  [the longest x21 13.2 us: collect_keys(): jnp.where(upper_half, jnp.concatenate([partner, key_block], axis=0), jnp....]
    reshape x8 -> x0, local copies, waits for them, and re-layouts: 12.9 us -> none  [the longest x4 12.5 us: collect_keys(): return key_block.reshape(CYCLE_MAX * tok_rows, piece_cols)]
  transfers between devices with their start and end apart: 29 -> 0, of which waited for: 28 -> 0; matrix products, arithmetic and copies ran while one was open for 2% -> 0% of each run, Pallas kernels for 0% -> 0%
where the time goes in v1:
time: 613 us; the launch traced here: 612 us
  Pallas kernels  594 us (97%)
  other arithmetic  9.09 us (1%)
  local copies, waits for them, and re-layouts  8.88 us (1%)
    pallas_call x1, Pallas kernels, body(): pl.pallas_call(functools.partial(kernel, chips, sections), out_shape=jax....  594 us

profile of v1, /device:TPU:31, one launch (start us, length us, event | category | flops | bytes accessed | tf_op | source)
XLA Modules:
  0.0 612.2 jit_solution(11232268076748674787)
XLA Ops:
  0.0 0.0 copy-start
  0.0 0.8 fusion.2
  0.8 0.9 select_reduce_fusion
  1.7 0.7 dynamic-slice_bitcast_fusion.1
  2.4 1.2 multiply_add_fusion
  3.5 0.6 broadcast_in_dim.35.code_k
  4.1 1.3 broadcast_in_dim.34.pos_k
  5.5 1.0 copy.11.code_q
  6.5 1.0 copy.10.pos_q
  7.5 1.1 slice_bitcast_fusion.7
  8.7 0.0 copy-done
  8.7 0.1 slice_bitcast_fusion.3
  8.8 0.0 copy-start.1
  8.8 1.3 maximum_maximum_fusion.wq_in
  10.0 0.4 copy-done.1
  10.4 0.1 slice_bitcast_fusion.1
  10.5 1.1 pad_maximum_fusion.wo_in
  11.6 1.9 fusion
  13.5 1.3 pad_maximum_fusion.1
  14.9 594.1 %shard_map.73 = bf16[4,128,2048]{2,1,0:T(8,128)(2,1)} custom-call(bf16[4,128,2048]{2,1,0:T(8,128)(2,1)} %x_ref.1, f32[1,2048]{1,0:T(1,128)} %gain_ref.1, bf16[2,256,1536]{2,1,0:T(8,128)(2,1)} %maximum_maximum_fusion.wq_in, bf16[2,256,1024]{2,1,0:T(8,128)(2,1)} %pad_maximum_fusion.wo_in, f32[4,256,128]{2,1,0:T(8,128)} %get-tuple-element.20.cos_ref, ...), custom_call_target="tpu_custom_call" | custom-call | tf_op jit(solution)/shard_map/pallas_call | solution.py:393
  609.0 3.2 copy.13
  (2 shorter events, 0.0 us)
Async XLA Ops:
  0.0 8.7 %copy-start = (bf16[1,256,3072]{2,1,0:T(8,128)(2,1)S(1)}, bf16[1,256,3072]{2,1,0:T(8,128)(2,1)}, u32[]{:S(2)}) copy-start(bf16[1,256,3072]{2,1,0:T(8,128)(2,1)} %param.9) | copy-start | bytes 4718596
  8.8 1.7 copy-start.1

commit v2 on v1

--- a/solution.py
+++ b/solution.py
@@ -204,6 +204,10 @@
     relay_weights(0)
     send_own(1)
 
+    @pl.when(section > 0)
+    def _():
+        relay_weights(1)
+
     def rope(values, m):
         return values * cos_ref[m] + pltpu.roll(values, HEAD_DIM // 2, 1) * sin_ref[m]
 
@@ -272,7 +276,7 @@
                 att[m, core, :, h * HEAD_DIM : (h + 1) * HEAD_DIM] = (combined / row_sum).astype(jnp.bfloat16)
             att_send(m, g).start()
 
-        @pl.when(m == 0)
+        @pl.when(first & (m == 0))
         def _():
             relay_weights(1)
 

time: 613 us -> 452 us (0.74)
  Pallas kernels: 594 us -> 434 us
    pallas_call x1, Pallas kernels: 594 us -> 434 us  [body(): pl.pallas_call(functools.partial(kernel, chips, sections), out_shape=jax....]
where the time goes in v2:
time: 452 us
  Pallas kernels  434 us (96%)
  other arithmetic  9.09 us (2%)
  local copies, waits for them, and re-layouts  8.88 us (2%)
    pallas_call x1, Pallas kernels, body(): pl.pallas_call(functools.partial(kernel, chips, sections), out_shape=jax....  434 us

profile of v2, /device:TPU:31, one launch (start us, length us, event | category | flops | bytes accessed | tf_op | source)
XLA Modules:
  0.0 451.8 jit_solution(17601898552203660838)
XLA Ops:
  0.0 0.0 copy-start
  0.0 0.8 fusion.2
  0.8 0.9 select_reduce_fusion
  1.7 0.7 dynamic-slice_bitcast_fusion.1
  2.4 1.2 multiply_add_fusion
  3.5 0.6 broadcast_in_dim.35.code_k
  4.1 1.3 broadcast_in_dim.34.pos_k
  5.5 1.0 copy.11.code_q
  6.5 1.0 copy.10.pos_q
  7.5 1.1 slice_bitcast_fusion.7
  8.7 0.0 copy-done
  8.7 0.1 slice_bitcast_fusion.3
  8.8 0.0 copy-start.1
  8.8 1.3 maximum_maximum_fusion.wq_in
  10.0 0.4 copy-done.1
  10.4 0.1 slice_bitcast_fusion.1
  10.5 1.1 pad_maximum_fusion.wo_in
  11.6 1.9 fusion
  13.5 1.3 pad_maximum_fusion.1
  14.9 433.7 %shard_map.73 = bf16[4,128,2048]{2,1,0:T(8,128)(2,1)} custom-call(bf16[4,128,2048]{2,1,0:T(8,128)(2,1)} %x_ref.1, f32[1,2048]{1,0:T(1,128)} %gain_ref.1, bf16[2,256,1536]{2,1,0:T(8,128)(2,1)} %maximum_maximum_fusion.wq_in, bf16[2,256,1024]{2,1,0:T(8,128)(2,1)} %pad_maximum_fusion.wo_in, f32[4,256,128]{2,1,0:T(8,128)} %get-tuple-element.20.cos_ref, ...), custom_call_target="tpu_custom_call" | custom-call | tf_op jit(solution)/shard_map/pallas_call | solution.py:397
  448.6 3.2 copy.13
  (2 shorter events, 0.0 us)
Async XLA Ops:
  0.0 8.7 %copy-start = (bf16[1,256,3072]{2,1,0:T(8,128)(2,1)S(1)}, bf16[1,256,3072]{2,1,0:T(8,128)(2,1)}, u32[]{:S(2)}) copy-start(bf16[1,256,3072]{2,1,0:T(8,128)(2,1)} %param.9) | copy-start | bytes 4718596
  8.8 1.7 copy-start.1
